TPU v7x, 32 devices: a whole 2x2x4 slice. The times are simulated.
32 devices in a mesh: dp: 8 (over z, y), mp: 4 (over x, core).
Axes of the slice: x: 2, y: 2, z: 4, core: 2. Of those that a mesh axis runs over, the one named last changes fastest.
Arguments:
- queries: bfloat16 [1024, 8192], P('dp', 'mp'), may hold values from -8 to 8
- tree_keys: bfloat16 [1024, 1024], P('dp', 'mp'), may hold values from -18 to 18
- tree_values: bfloat16 [1024, 1024], P('dp', 'mp'), may hold values from -6 to 6
- cache_keys: bfloat16 [16, 4096, 1024], P('dp', None, 'mp'), may hold values from -8 to 8
- cache_values: bfloat16 [16, 4096, 1024], P('dp', None, 'mp'), may hold values from -6 to 6
- cache_lens: int32 [16], P('dp'), may hold values from 1024 to 4096, as said below
- parents: int32 [16, 64], P('dp'), may hold values from -1 to 62, as said below
- accepted_nodes: int32 [16, 8], P('dp'), may hold values from 0 to 63, as said below
- residual: bfloat16 [1024, 8192], P('dp', 'mp'), may hold values from -1.796875 to 1.796875
- out_weight: bfloat16 [8192, 8192], P('mp', 'dp'), may hold values from -0.0625 to 0.0625
Outputs:
- tree_hidden: bfloat16 [1024, 8192], P('dp', 'mp')
- accepted_hidden: bfloat16 [128, 8192], P(None, 'mp')
Inputs may be any that keep to these rules, and one draw needn't show every extreme that they name: parents[r, 0] = -1 and 0 <= parents[r, i] < i for i >= 1. accepted_nodes[r, 0] = 0, the nodes of a row increase, and parents[r, accepted_nodes[r, a + 1]] = accepted_nodes[r, a]. `cache_lens`: some request has exactly 4096 filled positions.
All inputs are finite; a program needn't handle non-finite values.
Results may differ from a plain program's by a relative error of at most 0.015.
Values may be sent and summed in bfloat16 or wider, within the bound.
A program may use at most 64 MiB of HBM per device.

v0:
```python
import math
import jax
import jax.numpy as jnp
from jax import lax
from jax.sharding import PartitionSpec as P

HEADS = 64
KV_HEADS = 8
HD = 128
neg_large = -1e30


def ancestry(parents, node_count):
    positions = jnp.arange(node_count, dtype=jnp.int32)
    parent_hot = (parents[:, :, None] == positions[None, None, :]).astype(jnp.float32)
    reached = parent_hot + jnp.eye(node_count, dtype=jnp.float32)[None]
    for squaring in range((node_count - 1).bit_length()):
        reached = jnp.minimum(
            jnp.einsum("rij,rjk->rik", reached, reached, precision=lax.Precision.HIGHEST), 1.0
        )
    return reached > 0.5


def per_device(
    queries,
    tree_keys,
    tree_values,
    cache_keys,
    cache_values,
    cache_lens,
    parents,
    accepted_nodes,
    residual,
    out_weight,
):
    request_count = parents.shape[0]
    node_count = parents.shape[1]
    cache_length = cache_keys.shape[1]
    kv_local = tree_keys.shape[1] // HD
    group_size = HEADS // KV_HEADS
    scale_factor = 1.0 / math.sqrt(HD)
    query_grid = queries.reshape(request_count, node_count, kv_local, group_size, HD)
    tree_key_grid = tree_keys.reshape(request_count, node_count, kv_local, HD)
    tree_value_grid = tree_values.reshape(request_count, node_count, kv_local, HD)
    cache_key_grid = cache_keys.reshape(request_count, cache_length, kv_local, HD)
    cache_value_grid = cache_values.reshape(request_count, cache_length, kv_local, HD)
    ancestor = ancestry(parents, node_count)
    tree_scores = (
        jnp.einsum(
            "rnkgd,rjkd->rnkgj", query_grid, tree_key_grid, preferred_element_type=jnp.float32
        )
        * scale_factor
    )
    tree_scores = jnp.where(ancestor[:, :, None, None, :], tree_scores, neg_large)
    run_max = jnp.max(tree_scores, axis=-1)
    tree_weights = jnp.exp(tree_scores - run_max[..., None])
    run_sum = jnp.sum(tree_weights, axis=-1)
    run_acc = jnp.einsum(
        "rnkgj,rjkd->rnkgd",
        tree_weights.astype(jnp.bfloat16),
        tree_value_grid,
        preferred_element_type=jnp.float32,
    )
    block_len = min(512, cache_length)

    def absorb(block_number, state_now):
        old_max, old_sum, old_acc = state_now
        block_start = block_number * block_len
        key_block = lax.dynamic_slice_in_dim(cache_key_grid, block_start, block_len, 1)
        value_block = lax.dynamic_slice_in_dim(cache_value_grid, block_start, block_len, 1)
        block_scores = (
            jnp.einsum(
                "rnkgd,rpkd->rnkgp", query_grid, key_block, preferred_element_type=jnp.float32
            )
            * scale_factor
        )
        positions = block_start + jnp.arange(block_len, dtype=jnp.int32)
        live_keys = positions[None, :] < cache_lens[:, None]
        block_scores = jnp.where(live_keys[:, None, None, None, :], block_scores, neg_large)
        new_max = jnp.maximum(old_max, jnp.max(block_scores, axis=-1))
        block_weights = jnp.exp(block_scores - new_max[..., None])
        rescale = jnp.exp(old_max - new_max)
        new_sum = old_sum * rescale + jnp.sum(block_weights, axis=-1)
        new_acc = old_acc * rescale[..., None] + jnp.einsum(
            "rnkgp,rpkd->rnkgd",
            block_weights.astype(jnp.bfloat16),
            value_block,
            preferred_element_type=jnp.float32,
        )
        return (new_max, new_sum, new_acc)

    trip_count = cache_length // block_len
    run_max, run_sum, run_acc = lax.fori_loop(0, trip_count, absorb, (run_max, run_sum, run_acc))
    attended = (run_acc / run_sum[..., None]).astype(jnp.bfloat16)
    attended = attended.reshape(request_count * node_count, kv_local * group_size * HD)
    feature_share = residual.shape[1]
    all_rows = jnp.dot(
        lax.all_gather(attended, "dp", axis=0, tiled=True),
        out_weight,
        preferred_element_type=jnp.float32,
    )
    partial_sum = lax.all_to_all(
        all_rows.astype(jnp.bfloat16), "dp", split_axis=0, concat_axis=1, tiled=True
    ).astype(all_rows.dtype)
    head_total_sum = lax.psum(partial_sum.astype(jnp.bfloat16), "mp").astype(jnp.float32)
    own_share = lax.dynamic_slice_in_dim(
        head_total_sum, lax.axis_index("mp") * feature_share, feature_share, 1
    )
    tree_hidden = (residual.astype(jnp.float32) + own_share).astype(jnp.bfloat16)
    row_base = jnp.arange(request_count, dtype=jnp.int32)[:, None] * node_count
    picked_rows = (row_base + accepted_nodes).reshape(-1)
    picked_hidden = jnp.take(tree_hidden, picked_rows, axis=0)
    accepted_hidden = lax.all_gather(picked_hidden, "dp", axis=0, tiled=True)
    return (tree_hidden, accepted_hidden)


def solution(mesh):
    placed = (
        P("dp", "mp"),
        P("dp", "mp"),
        P("dp", "mp"),
        P("dp", None, "mp"),
        P("dp", None, "mp"),
        P("dp"),
        P("dp", None),
        P("dp", None),
        P("dp", "mp"),
        P("mp", "dp"),
    )
    return jax.shard_map(
        per_device,
        mesh=mesh,
        in_specs=placed,
        out_specs=(P("dp", "mp"), P(None, "mp")),
        check_vma=False,
    )
```

profile of v0, /device:TPU:0, one launch (start us, length us, event | category | flops | bytes accessed | tf_op | source)
XLA Modules:
  0.0 305.0 jit_solution(8466349382810361783)
XLA Ops:
  7.2 1.1 copy.42
  8.4 1.0 convolution_minimum_fusion.5
  9.8 0.2 convolution_minimum_fusion.2
  10.2 0.2 fusion.26
  10.5 0.9 reshape.112
  11.5 0.6 fusion.38
  12.2 0.3 fusion.27
  12.5 0.3 copy.21
  12.8 0.3 convolution_bitcast_fusion
  13.3 6.4 %copy.23 = bf16[2,4096,256]{1,2,0:T(8,128)(2,1)} copy(bf16[2,4096,256]{2,1,0:T(8,128)(2,1)} %param.15) | data formatting | bytes 8388608 | tf_op args[3]
  19.7 6.4 %copy.24 = bf16[2,4096,256]{1,2,0:T(8,128)(2,1)} copy(bf16[2,4096,256]{2,1,0:T(8,128)(2,1)} %param.16) | data formatting | bytes 8388608 | tf_op args[4]
  26.1 49.3 %while.17 = (s32[]{:T(128)}, f32[2,64,2,8]{1,3,2,0:T(8,128)S(1)}, f32[2,64,2,8]{1,3,2,0:T(8,128)S(1)}, f32[2,64,2,8,128]{4,1,3,2,0:T(8,128)S(1)}, s32[2]{0:T(128...) while((s32[]{:T(128)}, f32[2,64,2,8]{1,3,2,0:T(8,128)S(1)}, ...), condition=%wide.region_5.6_spmd, body=%wide.region_2.5_spmd.sunk | while | flops 548935168 | bytes 16392375 | solution.py:93
  26.2 1.8 bitcast_reduce_fusion.2
  28.0 1.7 fusion.61
  29.7 2.5 fusion.62
  32.3 1.8 bitcast_reduce_fusion.2
  34.2 1.7 fusion.61
  35.9 2.5 fusion.62
  38.5 1.8 bitcast_reduce_fusion.2
  40.3 1.7 fusion.61
  42.1 2.5 fusion.62
  44.7 1.8 bitcast_reduce_fusion.2
  46.5 1.7 fusion.61
  48.2 2.5 fusion.62
  50.8 1.8 bitcast_reduce_fusion.2
  52.7 1.7 fusion.61
  54.4 2.5 fusion.62
  57.0 1.8 bitcast_reduce_fusion.2
  58.9 1.7 fusion.61
  60.6 2.5 fusion.62
  63.2 1.8 bitcast_reduce_fusion.2
  65.0 1.7 fusion.61
  66.7 2.5 fusion.62
  69.3 1.8 bitcast_reduce_fusion.2
  71.2 1.7 fusion.61
  72.9 2.5 fusion.62
  75.4 0.3 divide_convert_fusion
  75.8 0.3 copy.29
  76.1 1.0 reshape.117
  77.2 75.6 %all-gather.2.cloned.1.call-done = bf16[1024,2048]{1,0:T(8,128)(2,1)} async-done(((bf16[128,2048]{1,0:T(8,128)(2,1)}), bf16[1024,2048]{1,0:T(8,128)(2,1)}) %all-gather.2.cloned.1.call-update) | async-done | bytes 4194320 | tf_op jit(solution)/shard_map/all_gather | solution.py:98
  152.8 7.9 %convolution_convert_fusion = bf16[1024,1024]{1,0:T(8,128)(2,1)S(1)} fusion(bf16[1024,2048]{1,0:T(8,128)(2,1)} %all-gather.2.cloned.1.call-done, bf16[2048,1024]{1,0:T(8,128)(2,1)} %param.21), kind=kOutput, calls=%fused_computation.27 | convolution fusion | flops 4296015872 | bytes 10485760 | tf_op jit(solution)/shard_map/dot_general | solution.py:97
  160.8 51.1 %all_to_all.19 = bf16[8,128,1024]{2,1,0:T(8,128)(2,1)S(1)} all-to-all(bf16[8,128,1024]{2,1,0:T(8,128)(2,1)S(1)} %bitcast.87), channel_id=1, replica_groups=mesh['dp'=8,'mp'=4] {'dp'}, dimensions={0} | all-to-all | bytes 4194304 | tf_op jit(solution)/shard_map/all_to_all | solution.py:102
  211.9 1.5 copy.41
  213.7 50.2 %all-reduce.2.cloned.1.call-done = bf16[128,8192]{1,0:T(8,128)(2,1)} async-done(((bf16[128,8192]{1,0:T(8,128)(2,1)}), bf16[128,8192]{1,0:T(8,128)(2,1)}) %all-reduce.2.cloned.1.call-update) | async-done | bytes 2097168 | tf_op jit(solution)/shard_map/psum | solution.py:105
  263.9 1.2 add_convert_fusion
  265.1 0.6 gather_fusion
  265.7 31.6 %all_gather.7 = bf16[128,2048]{1,0:T(8,128)(2,1)S(1)} all-gather(bf16[16,2048]{1,0:T(8,128)(2,1)S(1)} %broadcast_select_fusion), channel_id=1, replica_groups=mesh['dp'=8,'mp'=4] {'dp'}, dimensions={0}, use_global_device_ids=true | all-gather | bytes 589824 | tf_op jit(solution)/shard_map/all_gather | solution.py:113
  297.3 0.8 copy.67
  (70 shorter events, 2.3 us)
Async XLA Ops:
  7.2 5.6 %copy-start.2 = (bf16[128,256]{1,0:T(8,128)(2,1)S(1)}, bf16[128,256]{1,0:T(8,128)(2,1)}, u32[]{:S(2)}) copy-start(bf16[128,256]{1,0:T(8,128)(2,1)} %param.14) | copy-start | bytes 196612
  7.2 145.7 %all-gather.2.cloned.1.call-start = ((), (), s32[]{:S(2)}) async-start(), calls=%async_computation.1 | async-start | bytes 4718592 | tf_op jit(solution)/shard_map/all_gather | solution.py:98
  19.7 6.4 %copy-start.3 = (s32[2]{0:T(128)S(1)}, s32[2]{0:T(128)}, u32[]{:S(2)}) copy-start(s32[2]{0:T(128)} %param.17) | copy-start | bytes 28
  77.2 186.7 %all-reduce.2.cloned.1.call-start = ((), (), s32[]{:S(2)}) async-start(), calls=%async_computation.2 | async-start | bytes 4194304 | tf_op jit(solution)/shard_map/psum | solution.py:105
  211.9 1.5 copy-start.4
  211.9 51.9 %copy-start.1 = (bf16[128,2048]{1,0:T(8,128)(2,1)S(1)}, bf16[128,2048]{1,0:T(8,128)(2,1)}, u32[]{:S(2)}) copy-start(bf16[128,2048]{1,0:T(8,128)(2,1)} %param.20) | copy-start | bytes 1572868
  265.1 33.1 %copy-start = (bf16[128,2048]{1,0:T(8,128)(2,1)}, bf16[128,2048]{1,0:T(8,128)(2,1)S(1)}, u32[]{:S(2)}) copy-start(bf16[128,2048]{1,0:T(8,128)(2,1)S(1)} %add_convert_fusion) | copy-start | bytes 1572868
Sparse Core Ops, SparseCore 0:
  77.3 75.5 all-gather.1
  213.5 50.2 all-reduce.1
where the time goes:
time: 306 us; the launch traced here: 305 us
  waiting for transfers between devices  126 us (41%)
  blocking collectives  82.7 us (27%)
  matrix products  45.3 us (15%)
  local copies, waits for them, and re-layouts  20 us (7%)
  other arithmetic  16.3 us (5%)
  between operations  14.2 us (5%)
    all_gather x1, waiting for transfers between devices, per_device(): lax.all_gather(attended, 'dp', axis=0, tiled=True)  75.6 us
    all_to_all x1, blocking collectives, per_device(): lax.all_to_all(all_rows.astype(jnp.bfloat16), 'dp', split_axis=0, concat_...  51.1 us
    psum x1, waiting for transfers between devices, per_device(): lax.psum(partial_sum.astype(jnp.bfloat16), 'mp').astype(jnp.float32)  50.2 us
    all_gather x1, blocking collectives, per_device(): accepted_hidden = lax.all_gather(picked_hidden, 'dp', axis=0, tiled=True)  31.6 us
    dot_general x8, matrix products, absorb(): jnp.einsum('rnkgp,rpkd->rnkgd', block_weights.astype(jnp.bfloat16), value...  19.8 us
    unnamed x14, local copies, waits for them, and re-layouts  14.7 us
    dot_general x8, matrix products, absorb(): jnp.einsum('rnkgd,rpkd->rnkgp', query_grid, key_block, preferred_element_...  14.7 us
    reduce_sum x8, other arithmetic, absorb(): new_sum = old_sum * rescale + jnp.sum(block_weights, axis=-1)  13.6 us
  transfers between devices with their start and end apart: 2, of which 2 were waited for; matrix products, arithmetic and copies ran while one was open for 0% of the time, Pallas kernels for 0%

commit v1 on v0

--- a/solution.py
+++ b/solution.py
@@ -99,9 +99,19 @@
         out_weight,
         preferred_element_type=jnp.float32,
     )
-    partial_sum = lax.all_to_all(
-        all_rows.astype(jnp.bfloat16), "dp", split_axis=0, concat_axis=1, tiled=True
-    ).astype(all_rows.dtype)
+
+    def store_lanes_here(x_local, mesh_name, where_dim, along_dim=1):
+        return jnp.concatenate(
+            lax.all_to_all(
+                jnp.stack(jnp.split(x_local, lax.psum(1, mesh_name), axis=where_dim), axis=0),
+                mesh_name,
+                0,
+                0,
+            ),
+            axis=along_dim,
+        )
+
+    partial_sum = store_lanes_here(all_rows.astype(jnp.bfloat16), "dp", 0).astype(all_rows.dtype)
     head_total_sum = lax.psum(partial_sum.astype(jnp.bfloat16), "mp").astype(jnp.float32)
     own_share = lax.dynamic_slice_in_dim(
         head_total_sum, lax.axis_index("mp") * feature_share, feature_share, 1

time: 306 us -> 311 us (1.016)
  local copies, waits for them, and re-layouts: 20 us -> 25.2 us
    reshape x0 -> x2, local copies, waits for them, and re-layouts: none -> 6.53 us  [store_lanes_here(): jnp.concatenate(lax.all_to_all(jnp.stack(jnp.split(x_local, lax.psum(1, m...]
    unnamed x14 -> x23, local copies, waits for them, and re-layouts: 14.7 us -> 15.7 us
where the time goes in v1:
time: 311 us; the launch traced here: 310 us
  waiting for transfers between devices  125 us (40%)
  blocking collectives  82.7 us (27%)
  matrix products  45.3 us (15%)
  local copies, waits for them, and re-layouts  25.2 us (8%)
  other arithmetic  16.3 us (5%)
  between operations  14.3 us (5%)
    all_gather x1, waiting for transfers between devices, per_device(): lax.all_gather(attended, 'dp', axis=0, tiled=True)  75.6 us
    all_to_all x1, blocking collectives, store_lanes_here(): lax.all_to_all(jnp.stack(jnp.split(x_local, lax.psum(1, mesh_name), axis=...  51.1 us
    psum x1, waiting for transfers between devices, per_device(): lax.psum(partial_sum.astype(jnp.bfloat16), 'mp').astype(jnp.float32)  49.5 us
    all_gather x1, blocking collectives, per_device(): accepted_hidden = lax.all_gather(picked_hidden, 'dp', axis=0, tiled=True)  31.6 us
    dot_general x8, matrix products, absorb(): jnp.einsum('rnkgp,rpkd->rnkgd', block_weights.astype(jnp.bfloat16), value...  19.8 us
    unnamed x23, local copies, waits for them, and re-layouts  15.7 us
    dot_general x8, matrix products, absorb(): jnp.einsum('rnkgd,rpkd->rnkgp', query_grid, key_block, preferred_element_...  14.7 us
    reduce_sum x8, other arithmetic, absorb(): new_sum = old_sum * rescale + jnp.sum(block_weights, axis=-1)  13.6 us
  transfers between devices with their start and end apart: 2, of which 2 were waited for; matrix products, arithmetic and copies ran while one was open for 0% of the time, Pallas kernels for 0%

profile of v1, /device:TPU:0, one launch (start us, length us, event | category | flops | bytes accessed | tf_op | source)
XLA Modules:
  0.0 309.6 jit_solution(12215268202503081583)
XLA Ops:
  7.2 1.1 copy.41
  8.4 1.0 convolution_minimum_fusion.5
  10.2 0.2 fusion.26
  10.7 0.6 fusion.46
  11.4 0.3 fusion.27
  11.6 0.3 copy.20
  12.0 0.3 convolution_bitcast_fusion
  12.5 6.4 %copy.22 = bf16[2,4096,256]{1,2,0:T(8,128)(2,1)} copy(bf16[2,4096,256]{2,1,0:T(8,128)(2,1)} %param.15) | data formatting | bytes 8388608 | tf_op args[3]
  18.9 6.5 %copy.23 = bf16[2,4096,256]{1,2,0:T(8,128)(2,1)} copy(bf16[2,4096,256]{2,1,0:T(8,128)(2,1)} %param.16) | data formatting | bytes 8388608 | tf_op args[4]
  25.4 49.3 %while.17 = (s32[]{:T(128)}, f32[2,64,2,8]{1,3,2,0:T(8,128)S(1)}, f32[2,64,2,8]{1,3,2,0:T(8,128)S(1)}, f32[2,64,2,8,128]{4,1,3,2,0:T(8,128)S(1)}, s32[2]{0:T(128...) while((s32[]{:T(128)}, f32[2,64,2,8]{1,3,2,0:T(8,128)S(1)}, ...), condition=%wide.region_5.6_spmd, body=%wide.region_2.5_spmd.sunk | while | flops 548935168 | bytes 16392375 | solution.py:93
  25.5 1.8 bitcast_reduce_fusion.2
  27.4 1.7 fusion.69
  29.1 2.5 fusion.70
  31.7 1.8 bitcast_reduce_fusion.2
  33.5 1.7 fusion.69
  35.3 2.5 fusion.70
  37.8 1.8 bitcast_reduce_fusion.2
  39.7 1.7 fusion.69
  41.4 2.5 fusion.70
  44.0 1.8 bitcast_reduce_fusion.2
  45.9 1.7 fusion.69
  47.6 2.5 fusion.70
  50.2 1.8 bitcast_reduce_fusion.2
  52.0 1.7 fusion.69
  53.8 2.5 fusion.70
  56.4 1.8 bitcast_reduce_fusion.2
  58.2 1.7 fusion.69
  59.9 2.5 fusion.70
  62.5 1.8 bitcast_reduce_fusion.2
  64.4 1.7 fusion.69
  66.1 2.5 fusion.70
  68.7 1.8 bitcast_reduce_fusion.2
  70.5 1.7 fusion.69
  72.3 2.5 fusion.70
  74.8 0.3 divide_convert_fusion
  75.1 0.3 copy.28
  75.5 1.0 reshape.120
  76.6 75.6 %all-gather.2.cloned.1.call-done = bf16[1024,2048]{1,0:T(8,128)(2,1)} async-done(((bf16[128,2048]{1,0:T(8,128)(2,1)}), bf16[1024,2048]{1,0:T(8,128)(2,1)}) %all-gather.2.cloned.1.call-update) | async-done | bytes 4194320 | tf_op jit(solution)/shard_map/all_gather | solution.py:98
  152.2 7.9 %convolution_convert_fusion = bf16[1024,1024]{1,0:T(8,128)(2,1)S(1)} fusion(bf16[1024,2048]{1,0:T(8,128)(2,1)} %all-gather.2.cloned.1.call-done, bf16[2048,1024]{1,0:T(8,128)(2,1)} %param.21), kind=kOutput, calls=%fused_computation.27 | convolution fusion | flops 4296015872 | bytes 10485760 | tf_op jit(solution)/shard_map/dot_general | solution.py:97
  160.3 51.1 %all_to_all.5 = bf16[8,128,1024]{2,1,0:T(8,128)(2,1)S(1)} all-to-all(bf16[8,128,1024]{2,1,0:T(8,128)(2,1)S(1)} %fusion.29), channel_id=1, replica_groups=mesh['dp'=8,'mp'=4] {'dp'}, dimensions={0} | all-to-all | bytes 4194304 | tf_op jit(solution)/shard_map/all_to_all | solution.py:105
  211.5 2.4 copy.29
  213.9 4.1 %copy.30 = bf16[128,8192]{1,0:T(8,128)(2,1)} copy(bf16[128,8192]{0,1:T(8,128)(2,1)} %bitcast.113) | data formatting | bytes 4194304 | tf_op jit(solution)/shard_map/reshape | solution.py:104
  218.1 0.6 copy-done.5
  219.0 49.5 %all-reduce.2.cloned.1.call-done = bf16[128,8192]{1,0:T(8,128)(2,1)} async-done(((bf16[128,8192]{1,0:T(8,128)(2,1)}), bf16[128,8192]{1,0:T(8,128)(2,1)}) %all-reduce.2.cloned.1.call-update) | async-done | bytes 2097168 | tf_op jit(solution)/shard_map/psum | solution.py:115
  268.5 1.2 add_convert_fusion
  269.7 0.6 gather_fusion
  270.4 31.6 %all_gather.7 = bf16[128,2048]{1,0:T(8,128)(2,1)S(1)} all-gather(bf16[16,2048]{1,0:T(8,128)(2,1)S(1)} %broadcast_select_fusion), channel_id=1, replica_groups=mesh['dp'=8,'mp'=4] {'dp'}, dimensions={0}, use_global_device_ids=true | all-gather | bytes 589824 | tf_op jit(solution)/shard_map/all_gather | solution.py:123
  301.9 0.8 copy.73
  (81 shorter events, 2.7 us)
Async XLA Ops:
  7.2 3.4 %copy-start.2 = (bf16[128,256]{1,0:T(8,128)(2,1)S(1)}, bf16[128,256]{1,0:T(8,128)(2,1)}, u32[]{:S(2)}) copy-start(bf16[128,256]{1,0:T(8,128)(2,1)} %param.13) | copy-start | bytes 196612
  7.2 145.0 %all-gather.2.cloned.1.call-start = ((), (), s32[]{:S(2)}) async-start(), calls=%async_computation.1 | async-start | bytes 4718592 | tf_op jit(solution)/shard_map/all_gather | solution.py:98
  10.7 1.3 copy-start.3
  18.9 6.5 %copy-start.4 = (s32[2]{0:T(128)S(1)}, s32[2]{0:T(128)}, u32[]{:S(2)}) copy-start(s32[2]{0:T(128)} %param.17) | copy-start | bytes 28
  76.5 192.0 %all-reduce.2.cloned.1.call-start = ((), (), s32[]{:S(2)}) async-start(), calls=%async_computation.2 | async-start | bytes 4194304 | tf_op jit(solution)/shard_map/psum | solution.py:115
  218.0 0.7 copy-start.5
  218.0 50.5 %copy-start.1 = (bf16[128,2048]{1,0:T(8,128)(2,1)S(1)}, bf16[128,2048]{1,0:T(8,128)(2,1)}, u32[]{:S(2)}) copy-start(bf16[128,2048]{1,0:T(8,128)(2,1)} %param.20) | copy-start | bytes 1572868
  269.7 33.1 %copy-start = (bf16[128,2048]{1,0:T(8,128)(2,1)}, bf16[128,2048]{1,0:T(8,128)(2,1)S(1)}, u32[]{:S(2)}) copy-start(bf16[128,2048]{1,0:T(8,128)(2,1)S(1)} %add_convert_fusion) | copy-start | bytes 1572868
Sparse Core Ops, SparseCore 0:
  76.6 75.5 all-gather.1
  218.2 50.2 all-reduce.1
